TPU v7x, 32 devices: a whole 2x2x4 slice. The times are simulated.
32 devices in a mesh: batch: 16 (over z, y, core), gene: 2 (over x).
Axes of the slice: x: 2, y: 2, z: 4, core: 2. Of those that a mesh axis runs over, the one named last changes fastest.
Arguments:
- umi_counts: int32 [16384, 8192], P('batch', 'gene'), may hold values from 0 to 65535
- cell_donors: int32 [16384], P('batch'), may hold values from 0 to 127
- cell_types: int32 [16384], P('batch'), may hold values from 0 to 23
- live_cells: int32 [16], P('batch'), may hold values from 1 to 1024, 10240 in all
- dosages: int32 [128, 2048], P(None, 'batch'), may hold values from 0 to 2
Outputs:
- scores: bfloat16 [24, 8192, 2048], P(None, ('gene', 'batch'))
All inputs are finite; a program needn't handle non-finite values. No bound on the sum of `live_cells` on one device may be relied on, other than what follows from the above.
Results may differ from a plain program's by a relative error of at most 0.0069.
Values may be sent and summed in bfloat16 or wider, within the bound.
A program may use at most 128 MiB of HBM per device.

v0:
```python
import jax
import jax.numpy as jnp
from jax import lax
from jax.sharding import PartitionSpec as P

TYPES = 24
DONORS = 128


def one_hot_rows(group_ids, total_groups):
    columns = jnp.arange(total_groups, dtype=jnp.int32)
    return (group_ids[:, None] == columns[None, :]).astype(jnp.bfloat16)


def standardize_dosage(block_dosage):
    genotype = block_dosage.astype(jnp.float32)
    centred = genotype - jnp.mean(genotype, axis=0, keepdims=True)
    return (centred * lax.rsqrt(jnp.mean(centred * centred, axis=0, keepdims=True) + 1e-06)).astype(
        jnp.bfloat16
    )


def on_device(umi_counts, cell_donors, cell_types, live_cells, dosages):
    total_groups = TYPES * DONORS
    cell_slots = umi_counts.shape[0]
    genes_block = umi_counts.shape[1]
    batch_count = lax.axis_size("batch")
    genes_local = genes_block // batch_count
    slot_index = jnp.arange(cell_slots, dtype=jnp.int32)
    alive_mask = slot_index < live_cells[0]
    cell_group = jnp.where(alive_mask, cell_types * DONORS + cell_donors, -1)
    rounded = umi_counts.astype(jnp.bfloat16)
    exchanged = lax.all_to_all(rounded, "batch", split_axis=1, concat_axis=0, tiled=True)
    all_groups = lax.all_gather(cell_group, "batch", axis=0, tiled=True)
    block_rows = 4 * cell_slots
    block_turns = batch_count // 4

    def add_block(step_index, totals):
        block_counts = lax.dynamic_slice_in_dim(exchanged, step_index * block_rows, block_rows, 0)
        block_groups = lax.dynamic_slice_in_dim(all_groups, step_index * block_rows, block_rows, 0)
        table = one_hot_rows(block_groups, total_groups)
        return totals + lax.dot_general(
            block_counts, table, (((0,), (0,)), ((), ())), preferred_element_type=jnp.float32
        )

    pseudo = lax.fori_loop(
        0, block_turns, add_block, jnp.zeros((genes_local, total_groups), jnp.float32)
    )
    partial_library = jnp.sum(pseudo, axis=0)
    library = jnp.maximum(lax.psum(partial_library, ("batch", "gene")), 1.0)
    logged = jnp.log1p(10000.0 * pseudo / library[None, :]).reshape(genes_local, TYPES, DONORS)
    centred = logged - jnp.mean(logged, axis=2, keepdims=True)
    standard = (
        centred * lax.rsqrt(jnp.mean(centred * centred, axis=2, keepdims=True) + 1e-06)
    ).astype(jnp.bfloat16)
    standard_rows = jnp.transpose(standard, (1, 0, 2)).reshape(TYPES * genes_local, DONORS)
    factor = DONORS ** (-0.5)
    geno_local = standardize_dosage(dosages)
    geno_piece = lax.all_gather(geno_local, "batch", axis=1, tiled=True)
    product = jnp.dot(standard_rows, geno_piece, preferred_element_type=jnp.float32) * factor
    return product.reshape(TYPES, genes_local, geno_piece.shape[1]).astype(jnp.bfloat16)


def solution(mesh):
    placed = (P("batch", "gene"), P("batch"), P("batch"), P("batch"), P(None, "batch"))
    return jax.shard_map(
        on_device,
        mesh=mesh,
        in_specs=placed,
        out_specs=P(None, ("gene", "batch"), None),
        check_vma=False,
    )
```

profile of v0, /device:TPU:14, one launch (start us, length us, event | category | flops | bytes accessed | tf_op | source)
XLA Modules:
  0.0 357.4 jit_solution(3607183109049914522)
XLA Ops:
  0.0 9.0 %convert_element_type.21 = bf16[1024,4096]{1,0:T(8,128)(2,1)} convert(s32[1024,4096]{1,0:T(8,128)} %param.7) | non-fusion elementwise | flops 4194304 | bytes 25165824 | tf_op jit(solution)/shard_map/convert_element_type | solution.py:32
  9.0 7.4 %copy.16 = bf16[128,16,8,256]{3,2,0,1:T(8,128)(2,1)} copy(bf16[128,16,8,256]{3,2,1,0:T(8,128)(2,1)} %bitcast.19) | data formatting | bytes 16777216 | tf_op jit(solution)/shard_map/all_to_all | solution.py:33
  16.5 0.0 copy-start.2
  16.5 0.0 copy-start.3
  16.5 0.0 copy-start.1
  16.5 6.4 %all-to-all-start = ((bf16[1024,16,256]{2,0,1:T(8,128)(2,1)}), bf16[1024,16,256]{2,0,1:T(8,128)(2,1)}, u32[]{:S(2)}, u32[]{:S(2)}) async-start(bf16[1024,16,256]{2,0,1:T(8,128)(2,1)} %bitcast.20), calls=%async_computation | async-start | bytes 16777216 | tf_op jit(solution)/shard_map/all_to_all | solution.py:33
  23.5 0.0 copy-done.2
  23.5 0.0 copy-done.3
  23.5 191.0 %all_gather.6 = s32[16384]{0:T(1024)S(1)} all-gather(s32[1024]{0:T(1024)S(1)} %add_select_fusion), channel_id=1, replica_groups=mesh['batch'=16,'gene'=2] {'batch'}, dimensions={0}, use_global_device_ids=true | all-gather | bytes 69632 | tf_op jit(solution)/shard_map/all_gather | solution.py:34
  214.5 0.0 copy-done.1
  214.6 18.3 %all_gather.7 = bf16[128,2048]{1,0:T(8,128)(2,1)} all-gather(bf16[128,128]{1,0:T(8,128)(2,1)S(1)} %multiply_convert_fusion.2), channel_id=1, replica_groups=mesh['batch'=16,'gene'=2] {'batch'}, dimensions={1}, use_global_device_ids=true | all-gather | bytes 557056 | tf_op jit(solution)/shard_map/all_gather | solution.py:59
  232.9 0.0 all-to-all-done
  232.9 57.8 %while.14 = (s32[]{:T(128)}, f32[256,3072]{1,0:T(8,128)S(1)}, bf16[16384,256]{1,0:T(8,128)(2,1)}, s32[16384]{0:T(1024)S(1)}, s32[]{:T(128)}, /*index=5*/s32[]{:T(128)}, s32[]{:T(128)}, s32[]{:T(128)}) while((s32[]{:T(128)}, f32[256,3072]{1,0:T(8,128)S(1)}, bf16[16384,256]{1,0:T(8,128)(2,1)}, s32[16384]{0:T(1024)S(1)}, s32[]{:T(128)}, ...), condition=%wide.region_1.2_spmd.clone, body=%wide.region_0.1_spmd.clone.sunk | while | flops 6456606720 | bytes 8437917 | solution.py:46
  232.9 14.4 %fusion.11 = f32[256,3072]{1,0:T(8,128)S(1)} fusion(s32[4096]{0:T(1024)S(1)} %dynamic_slice.21, f32[256,3072]{1,0:T(8,128)S(1)} %get-tuple-element.142, bf16[16384,256]{1,0:T(8,128)(2,1)} %get-tuple-element.151, s32[]{:T(128)S(6)} %select_n.16, pred[]{:T(512)S(6)} %compare.3), kind=kOutput, calls=%fused_computation.3.clone.1 | convolution fusion | flops 6456606720 | bytes 8404997 | tf_op jit(solution)/shard_map/while/body/eval_jaxpr/dot_general | solution.py:42
  247.4 14.4 %fusion.11 = f32[256,3072]{1,0:T(8,128)S(1)} fusion(s32[4096]{0:T(1024)S(1)} %dynamic_slice.21, f32[256,3072]{1,0:T(8,128)S(1)} %get-tuple-element.142, bf16[16384,256]{1,0:T(8,128)(2,1)} %get-tuple-element.151, s32[]{:T(128)S(6)} %select_n.16, pred[]{:T(512)S(6)} %compare.3), kind=kOutput, calls=%fused_computation.3.clone.1 | convolution fusion | flops 6456606720 | bytes 8404997 | tf_op jit(solution)/shard_map/while/body/eval_jaxpr/dot_general | solution.py:42
  261.8 14.4 %fusion.11 = f32[256,3072]{1,0:T(8,128)S(1)} fusion(s32[4096]{0:T(1024)S(1)} %dynamic_slice.21, f32[256,3072]{1,0:T(8,128)S(1)} %get-tuple-element.142, bf16[16384,256]{1,0:T(8,128)(2,1)} %get-tuple-element.151, s32[]{:T(128)S(6)} %select_n.16, pred[]{:T(512)S(6)} %compare.3), kind=kOutput, calls=%fused_computation.3.clone.1 | convolution fusion | flops 6456606720 | bytes 8404997 | tf_op jit(solution)/shard_map/while/body/eval_jaxpr/dot_general | solution.py:42
  276.3 14.4 %fusion.11 = f32[256,3072]{1,0:T(8,128)S(1)} fusion(s32[4096]{0:T(1024)S(1)} %dynamic_slice.21, f32[256,3072]{1,0:T(8,128)S(1)} %get-tuple-element.142, bf16[16384,256]{1,0:T(8,128)(2,1)} %get-tuple-element.151, s32[]{:T(128)S(6)} %select_n.16, pred[]{:T(512)S(6)} %compare.3), kind=kOutput, calls=%fused_computation.3.clone.1 | convolution fusion | flops 6456606720 | bytes 8404997 | tf_op jit(solution)/shard_map/while/body/eval_jaxpr/dot_general | solution.py:42
  290.7 2.5 copy.12
  293.3 0.2 reduce_sum.45
  293.4 44.2 %psum.7 = f32[3072]{0:T(1024)S(1)} all-reduce(f32[3072]{0:T(1024)S(1)} %reduce_sum.45), channel_id=1, replica_groups=mesh['batch'=16,'gene'=2] {'batch','gene'}, use_global_device_ids=true, to_apply=%region_3.4 | all-reduce | flops 3072 | bytes 24576 | tf_op jit(solution)/shard_map/psum | solution.py:50
  337.7 3.1 divide_log-plus-one_fusion
  340.8 0.2 reduce_sum.46
  341.1 0.4 multiply_reduce_fusion
  341.5 1.6 fusion.5
  343.1 0.0 copy-start
  343.1 2.0 copy.13
  345.0 0.0 copy-done
  345.0 12.4 %multiply_convert_fusion = bf16[6144,2048]{1,0:T(8,128)(2,1)} fusion(bf16[6144,128]{1,0:T(8,128)(2,1)S(1)} %bitcast.21, bf16[128,2048]{1,0:T(8,128)(2,1)S(1)} %copy-done), kind=kOutput, calls=%fused_computation.6 | convolution fusion | flops 3246391296 | bytes 27262976 | tf_op jit(solution)/shard_map/dot_general | solution.py:60
  (14 shorter events, 0.2 us)
Async XLA Ops:
  16.5 7.0 %copy-start.2 = (s32[1024]{0:T(1024)S(1)}, s32[1024]{0:T(1024)}, u32[]{:S(2)}) copy-start(s32[1024]{0:T(1024)} %param.8) | copy-start | bytes 12292
  16.5 7.0 %copy-start.3 = (s32[1024]{0:T(1024)S(1)}, s32[1024]{0:T(1024)}, u32[]{:S(2)}) copy-start(s32[1024]{0:T(1024)} %param.9) | copy-start | bytes 12292
  16.5 198.0 %copy-start.1 = (s32[128,128]{1,0:T(8,128)S(1)}, s32[128,128]{1,0:T(8,128)}, u32[]{:S(2)}) copy-start(s32[128,128]{1,0:T(8,128)} %param.11) | copy-start | bytes 196612
  16.5 216.4 %all-to-all-start = ((bf16[1024,16,256]{2,0,1:T(8,128)(2,1)}), bf16[1024,16,256]{2,0,1:T(8,128)(2,1)}, u32[]{:S(2)}, u32[]{:S(2)}) async-start(bf16[1024,16,256]{2,0,1:T(8,128)(2,1)} %bitcast.20), calls=%async_computation | async-start | bytes 16777216 | tf_op jit(solution)/shard_map/all_to_all | solution.py:33
  343.1 2.0 copy-start
where the time goes:
time: 358 us; the launch traced here: 357 us
  blocking collectives  253 us (71%)
  matrix products  70 us (20%)
  other arithmetic  14.7 us (4%)
  local copies, waits for them, and re-layouts  12 us (3%)
  starting transfers between devices  6.37 us (2%)
    all_gather x1, blocking collectives, on_device(): all_groups = lax.all_gather(cell_group, 'batch', axis=0, tiled=True)  191 us
    dot_general x4, matrix products, add_block(): lax.dot_general(block_counts, table, (((0,), (0,)), ((), ())), preferred_...  57.6 us
    psum x1, blocking collectives, on_device(): library = jnp.maximum(lax.psum(partial_library, ('batch', 'gene')), 1.0)  44.2 us
    all_gather x1, blocking collectives, on_device(): geno_piece = lax.all_gather(geno_local, 'batch', axis=1, tiled=True)  18.3 us
    dot_general x1, matrix products, on_device(): jnp.dot(standard_rows, geno_piece, preferred_element_type=jnp.float32)  12.4 us
    convert_element_type x1, other arithmetic, on_device(): rounded = umi_counts.astype(jnp.bfloat16)  9.05 us
    all_to_all x1, local copies, waits for them, and re-layouts, on_device(): lax.all_to_all(rounded, 'batch', split_axis=1, concat_axis=0, tiled=True)  7.43 us
  transfers between devices with their start and end apart: 1, of which 0 were waited for; matrix products, arithmetic and copies ran while one was open for 0% of the time, Pallas kernels for 0%

commit v1 on v0

--- a/solution.py
+++ b/solution.py
@@ -2,6 +2,7 @@
 import jax.numpy as jnp
 from jax import lax
 from jax.sharding import PartitionSpec as P
+from jax.lax import axis_index, axis_size, ppermute
 
 TYPES = 24
 DONORS = 128
@@ -56,7 +57,16 @@
     standard_rows = jnp.transpose(standard, (1, 0, 2)).reshape(TYPES * genes_local, DONORS)
     factor = DONORS ** (-0.5)
     geno_local = standardize_dosage(dosages)
-    geno_piece = lax.all_gather(geno_local, "batch", axis=1, tiled=True)
+    count_all = axis_size("batch")
+    seen = [(hop_no, (hop_no + 1) % count_all) for hop_no in range(count_all)]
+    z1 = [None] * count_all
+    z1[count_all - 1] = geno_local
+    for j in range(count_all - 2, -1, -1):
+        z1[j] = ppermute(z1[j + 1], axis_name="batch", perm=seen)
+    e_next = jnp.concatenate(z1, axis=1)
+    r2 = axis_index("batch")
+    earlier = (r2 + 1) * geno_local.shape[1]
+    geno_piece = jnp.roll(e_next, earlier, axis=1)
     product = jnp.dot(standard_rows, geno_piece, preferred_element_type=jnp.float32) * factor
     return product.reshape(TYPES, genes_local, geno_piece.shape[1]).astype(jnp.bfloat16)
 

time: 358 us -> 432 us (1.21)
  blocking collectives: 253 us -> 56.2 us
  starting transfers between devices: 6.37 us -> 196 us
  waiting for transfers between devices: 0.01 us -> 45.9 us
  local copies, waits for them, and re-layouts: 12 us -> 43 us
    ppermute x0 -> x15, starting transfers between devices: none -> 189 us  [on_device(): z1[j] = ppermute(z1[j + 1], axis_name='batch', perm=seen)]
    all_gather x1, blocking collectives: 191 us -> 16.1 us  [on_device(): all_groups = lax.all_gather(cell_group, 'batch', axis=0, tiled=True)]
    ppermute x0 -> x15, waiting for transfers between devices: none -> 45.9 us  [on_device(): z1[j] = ppermute(z1[j + 1], axis_name='batch', perm=seen)]
    unnamed x8 -> x46, local copies, waits for them, and re-layouts: 0.01 us -> 31 us
    all_gather x1 -> x0, blocking collectives: 18.3 us -> none  [on_device(): geno_piece = lax.all_gather(geno_local, 'batch', axis=1, tiled=True)]
  transfers between devices with their start and end apart: 1 -> 16, of which waited for: 0 -> 14; matrix products, arithmetic and copies ran while one was open for 0% -> 7% of each run, Pallas kernels for 0% -> 0%
where the time goes in v1:
time: 432 us; the launch traced here: 429 us
  starting transfers between devices  196 us (45%)
  matrix products  71.1 us (16%)
  blocking collectives  56.2 us (13%)
  waiting for transfers between devices  45.9 us (11%)
  local copies, waits for them, and re-layouts  43 us (10%)
  other arithmetic  15.9 us (4%)
    ppermute x15, starting transfers between devices, on_device(): z1[j] = ppermute(z1[j + 1], axis_name='batch', perm=seen)  189 us
    dot_general x4, matrix products, add_block(): lax.dot_general(block_counts, table, (((0,), (0,)), ((), ())), preferred_...  57.6 us
    ppermute x15, waiting for transfers between devices, on_device(): z1[j] = ppermute(z1[j + 1], axis_name='batch', perm=seen)  45.9 us
    psum x1, blocking collectives, on_device(): library = jnp.maximum(lax.psum(partial_library, ('batch', 'gene')), 1.0)  40 us
    unnamed x46, local copies, waits for them, and re-layouts  31 us
    all_gather x1, blocking collectives, on_device(): all_groups = lax.all_gather(cell_group, 'batch', axis=0, tiled=True)  16.1 us
    dot_general x1, matrix products, on_device(): jnp.dot(standard_rows, geno_piece, preferred_element_type=jnp.float32)  13.4 us
    convert_element_type x1, other arithmetic, on_device(): rounded = umi_counts.astype(jnp.bfloat16)  9.05 us
  transfers between devices with their start and end apart: 16, of which 14 were waited for; matrix products, arithmetic and copies ran while one was open for 7% of the time, Pallas kernels for 0%

profile of v1, /device:TPU:14, one launch (start us, length us, event | category | flops | bytes accessed | tf_op | source)
XLA Modules:
  0.0 428.7 jit_solution(10993102229927365934)
XLA Ops:
  0.0 9.0 %convert_element_type.21 = bf16[1024,4096]{1,0:T(8,128)(2,1)} convert(s32[1024,4096]{1,0:T(8,128)} %param.7) | non-fusion elementwise | flops 4194304 | bytes 25165824 | tf_op jit(solution)/shard_map/convert_element_type | solution.py:33
  9.0 7.5 %copy.16 = bf16[128,16,8,256]{3,2,0,1:T(8,128)(2,1)} copy(bf16[128,16,8,256]{3,2,1,0:T(8,128)(2,1)} %bitcast.18) | data formatting | bytes 16777216 | tf_op jit(solution)/shard_map/all_to_all | solution.py:34
  16.5 6.4 %all-to-all-start = ((bf16[1024,16,256]{2,0,1:T(8,128)(2,1)}), bf16[1024,16,256]{2,0,1:T(8,128)(2,1)}, u32[]{:S(2)}, u32[]{:S(2)}) async-start(bf16[1024,16,256]{2,0,1:T(8,128)(2,1)} %bitcast.19), calls=%async_computation | async-start | bytes 16777216 | tf_op jit(solution)/shard_map/all_to_all | solution.py:34
  23.2 35.3 %collective-permute-done = bf16[128,128]{1,0:T(8,128)(2,1)S(1)} collective-permute-done((bf16[128,128]{1,0:T(8,128)(2,1)S(1)}, bf16[128,128]{1,0:T(8,128)(2,1)S(1)}, u32[]{:S(2)}, u32[]{:S(2)}) %collective-permute-start) | collective-permute-done | bytes 32800 | tf_op jit(solution)/shard_map/ppermute | solution.py:65
  58.4 145.2 %collective-permute-start.1 = (bf16[128,128]{1,0:T(8,128)(2,1)S(1)}, bf16[128,128]{1,0:T(8,128)(2,1)S(1)}, u32[]{:S(2)}, u32[]{:S(2)}) collective-permute-start(bf16[128,128]{1,0:T(8,128)(2,1)S(1)} %collective-permute-done), channel_id=1, source_target_pairs={{0,2},{2,4},{4,6},{6,8},{8,10},{10,12},{12,14},{14,16},{16,18},{18... | collective-permute-start | bytes 98312 | tf_op jit(solution)/shard_map/ppermute | solution.py:65
  204.5 3.5 collective-permute-start.2
  208.9 3.4 collective-permute-start.3
  213.2 3.4 collective-permute-start.4
  217.4 3.4 collective-permute-start.5
  221.6 3.4 collective-permute-start.6
  225.9 3.4 collective-permute-start.7
  230.1 3.4 collective-permute-start.8
  234.4 3.4 collective-permute-start.9
  238.6 3.4 collective-permute-start.10
  243.4 3.4 collective-permute-start.11
  248.3 3.4 collective-permute-start.12
  253.1 3.4 collective-permute-start.13
  257.5 3.2 collective-permute-start.14
  260.8 16.1 %all_gather.3 = s32[16384]{0:T(1024)S(1)} all-gather(s32[1024]{0:T(1024)S(1)} %add_select_fusion), channel_id=1, replica_groups=mesh['batch'=16,'gene'=2] {'batch'}, dimensions={0}, use_global_device_ids=true | all-gather | bytes 69632 | tf_op jit(solution)/shard_map/all_gather | solution.py:35
  283.8 1.4 constant_dynamic-update-slice_fusion.26
  296.3 1.4 constant_dynamic-update-slice_fusion.12
  307.4 57.8 %while.14 = (s32[]{:T(128)}, f32[256,3072]{1,0:T(8,128)S(1)}, bf16[16384,256]{1,0:T(8,128)(2,1)}, s32[16384]{0:T(1024)S(1)}, s32[]{:T(128)}, /*index=5*/s32[]{:T(128)}, s32[]{:T(128)}, s32[]{:T(128)}) while((s32[]{:T(128)}, f32[256,3072]{1,0:T(8,128)S(1)}, bf16[16384,256]{1,0:T(8,128)(2,1)}, s32[16384]{0:T(1024)S(1)}, s32[]{:T(128)}, ...), condition=%wide.region_1.2_spmd.clone, body=%wide.region_0.1_spmd.clone.sunk | while | flops 6456606720 | bytes 8437917 | solution.py:47
  307.4 14.4 %fusion.12 = f32[256,3072]{1,0:T(8,128)S(1)} fusion(s32[4096]{0:T(1024)S(1)} %dynamic_slice.28, f32[256,3072]{1,0:T(8,128)S(1)} %get-tuple-element.142, bf16[16384,256]{1,0:T(8,128)(2,1)} %get-tuple-element.151, s32[]{:T(128)S(6)} %select_n.31, pred[]{:T(512)S(6)} %compare.4), kind=kOutput, calls=%fused_computation.3.clone.1 | convolution fusion | flops 6456606720 | bytes 8404997 | tf_op jit(solution)/shard_map/while/body/eval_jaxpr/dot_general | solution.py:43
  321.9 14.4 %fusion.12 = f32[256,3072]{1,0:T(8,128)S(1)} fusion(s32[4096]{0:T(1024)S(1)} %dynamic_slice.28, f32[256,3072]{1,0:T(8,128)S(1)} %get-tuple-element.142, bf16[16384,256]{1,0:T(8,128)(2,1)} %get-tuple-element.151, s32[]{:T(128)S(6)} %select_n.31, pred[]{:T(512)S(6)} %compare.4), kind=kOutput, calls=%fused_computation.3.clone.1 | convolution fusion | flops 6456606720 | bytes 8404997 | tf_op jit(solution)/shard_map/while/body/eval_jaxpr/dot_general | solution.py:43
  336.3 14.4 %fusion.12 = f32[256,3072]{1,0:T(8,128)S(1)} fusion(s32[4096]{0:T(1024)S(1)} %dynamic_slice.28, f32[256,3072]{1,0:T(8,128)S(1)} %get-tuple-element.142, bf16[16384,256]{1,0:T(8,128)(2,1)} %get-tuple-element.151, s32[]{:T(128)S(6)} %select_n.31, pred[]{:T(512)S(6)} %compare.4), kind=kOutput, calls=%fused_computation.3.clone.1 | convolution fusion | flops 6456606720 | bytes 8404997 | tf_op jit(solution)/shard_map/while/body/eval_jaxpr/dot_general | solution.py:43
  350.8 14.4 %fusion.12 = f32[256,3072]{1,0:T(8,128)S(1)} fusion(s32[4096]{0:T(1024)S(1)} %dynamic_slice.28, f32[256,3072]{1,0:T(8,128)S(1)} %get-tuple-element.142, bf16[16384,256]{1,0:T(8,128)(2,1)} %get-tuple-element.151, s32[]{:T(128)S(6)} %select_n.31, pred[]{:T(512)S(6)} %compare.4), kind=kOutput, calls=%fused_computation.3.clone.1 | convolution fusion | flops 6456606720 | bytes 8404997 | tf_op jit(solution)/shard_map/while/body/eval_jaxpr/dot_general | solution.py:43
  365.2 2.6 copy.12
  368.0 40.0 %psum.7 = f32[3072]{0:T(1024)S(1)} all-reduce(f32[3072]{0:T(1024)S(1)} %reduce_sum.45), channel_id=1, replica_groups=mesh['batch'=16,'gene'=2] {'batch','gene'}, use_global_device_ids=true, to_apply=%region_3.4 | all-reduce | flops 3072 | bytes 24576 | tf_op jit(solution)/shard_map/psum | solution.py:51
  408.0 3.1 divide_log-plus-one_fusion
  411.8 1.6 fusion.5
  413.4 1.9 copy.13
  415.3 13.4 %multiply_convert_fusion = bf16[6144,2048]{1,0:T(8,128)(2,1)} fusion(bf16[6144,128]{1,0:T(8,128)(2,1)S(1)} %bitcast.20, bf16[128,4096]{1,0:T(8,128)(2,1)} %constant_dynamic-update-slice_fusion, s32[]{:T(128)S(6)} %select_n.27), kind=kOutput, calls=%fused_computation.6 | convolution fusion | flops 3246391296 | bytes 27262980 | tf_op jit(solution)/shard_map/dot_general | solution.py:70
  (79 shorter events, 41.3 us)
Async XLA Ops:
  16.5 6.4 %copy-start = (s32[128,128]{1,0:T(8,128)S(1)}, s32[128,128]{1,0:T(8,128)}, u32[]{:S(2)}) copy-start(s32[128,128]{1,0:T(8,128)} %param.11) | copy-start | bytes 196612
  16.5 244.3 %copy-start.6 = (s32[1024]{0:T(1024)S(1)}, s32[1024]{0:T(1024)}, u32[]{:S(2)}) copy-start(s32[1024]{0:T(1024)} %param.8) | copy-start | bytes 12292
  16.5 244.3 %copy-start.7 = (s32[1024]{0:T(1024)S(1)}, s32[1024]{0:T(1024)}, u32[]{:S(2)}) copy-start(s32[1024]{0:T(1024)} %param.9) | copy-start | bytes 12292
  16.5 290.9 %all-to-all-start = ((bf16[1024,16,256]{2,0,1:T(8,128)(2,1)}), bf16[1024,16,256]{2,0,1:T(8,128)(2,1)}, u32[]{:S(2)}, u32[]{:S(2)}) async-start(bf16[1024,16,256]{2,0,1:T(8,128)(2,1)} %bitcast.19), calls=%async_computation | async-start | bytes 16777216 | tf_op jit(solution)/shard_map/all_to_all | solution.py:34
  23.0 35.4 %collective-permute-start = (bf16[128,128]{1,0:T(8,128)(2,1)S(1)}, bf16[128,128]{1,0:T(8,128)(2,1)S(1)}, u32[]{:S(2)}, u32[]{:S(2)}) collective-permute-start(bf16[128,128]{1,0:T(8,128)(2,1)S(1)} %multiply_convert_fusion.2), channel_id=1, source_target_pairs={{0,2},{2,4},{4,6},{6,8},{8,10},{10,12},{12,14},{14,16},{16,18},{18... | collective-permute-start | bytes 98312 | tf_op jit(solution)/shard_map/ppermute | solution.py:65
  58.4 146.1 %collective-permute-start.1 = (bf16[128,128]{1,0:T(8,128)(2,1)S(1)}, bf16[128,128]{1,0:T(8,128)(2,1)S(1)}, u32[]{:S(2)}, u32[]{:S(2)}) collective-permute-start(bf16[128,128]{1,0:T(8,128)(2,1)S(1)} %collective-permute-done), channel_id=1, source_target_pairs={{0,2},{2,4},{4,6},{6,8},{8,10},{10,12},{12,14},{14,16},{16,18},{18... | collective-permute-start | bytes 98312 | tf_op jit(solution)/shard_map/ppermute | solution.py:65
  204.5 4.4 %collective-permute-start.2 = (bf16[128,128]{1,0:T(8,128)(2,1)S(1)}, bf16[128,128]{1,0:T(8,128)(2,1)S(1)}, u32[]{:S(2)}, u32[]{:S(2)}) collective-permute-start(bf16[128,128]{1,0:T(8,128)(2,1)S(1)} %collective-permute-done.1), channel_id=1, source_target_pairs={{0,2},{2,4},{4,6},{6,8},{8,10},{10,12},{12,14},{14,16},{16,18},{18... | collective-permute-start | bytes 98312 | tf_op jit(solution)/shard_map/ppermute | solution.py:65
  208.9 4.2 collective-permute-start.3
  213.2 4.2 collective-permute-start.4
  217.4 4.2 collective-permute-start.5
  221.6 4.2 collective-permute-start.6
  225.9 4.2 collective-permute-start.7
  230.1 4.2 collective-permute-start.8
  234.4 26.5 %copy-start.1 = (bf16[128,128]{1,0:T(8,128)(2,1)}, bf16[128,128]{1,0:T(8,128)(2,1)S(1)}, u32[]{:S(2)}) copy-start(bf16[128,128]{1,0:T(8,128)(2,1)S(1)} %collective-permute-done.8) | copy-start | bytes 98308
  234.4 4.2 collective-permute-start.9
  238.6 22.2 %copy-start.2 = (bf16[128,128]{1,0:T(8,128)(2,1)}, bf16[128,128]{1,0:T(8,128)(2,1)S(1)}, u32[]{:S(2)}) copy-start(bf16[128,128]{1,0:T(8,128)(2,1)S(1)} %collective-permute-done.9) | copy-start | bytes 98308
  238.6 4.2 collective-permute-start.10
  242.8 0.6 copy-start.3
  243.4 4.2 collective-permute-start.11
  247.7 0.6 copy-start.4
  248.3 4.2 collective-permute-start.12
  252.5 0.6 copy-start.5
  253.1 4.4 %collective-permute-start.13 = (bf16[128,128]{1,0:T(8,128)(2,1)S(1)}, bf16[128,128]{1,0:T(8,128)(2,1)}, u32[]{:S(2)}, u32[]{:S(2)}) collective-permute-start(bf16[128,128]{1,0:T(8,128)(2,1)S(1)} %collective-permute-done.12), channel_id=1, source_target_pairs={{0,2},{2,4},{4,6},{6,8},{8,10},{10,12},{12,14},{14,16},{16,18},{18... | collective-permute-start | bytes 98312 | tf_op jit(solution)/shard_map/ppermute | solution.py:65
  257.5 19.5 %collective-permute-start.14 = (bf16[128,128]{1,0:T(8,128)(2,1)}, bf16[128,128]{1,0:T(8,128)(2,1)}, u32[]{:S(2)}, u32[]{:S(2)}) collective-permute-start(bf16[128,128]{1,0:T(8,128)(2,1)} %collective-permute-done.13), channel_id=1, source_target_pairs={{0,2},{2,4},{4,6},{6,8},{8,10},{10,12},{12,14},{14,16},{16,18},{18... | collective-permute-start | bytes 98312 | tf_op jit(solution)/shard_map/ppermute | solution.py:65
